TPU v7x, 32 devices: a whole 2x2x4 slice. The times are simulated.
32 devices in a mesh: ep: 4 (over y, core), fsdp: 8 (over z, x).
Axes of the slice: x: 2, y: 2, z: 4, core: 2. Of those that a mesh axis runs over, the one named last changes fastest.
Arguments:
- master_down: float32 [16, 6400, 4096], P('ep', None, 'fsdp'), may hold values from -0.109375 to 0.109375
- second_down: bfloat16 [16, 6400, 4096], P('ep', None, 'fsdp'), may hold values from -0.0390625 to 0.0390625
- router_weight: float32 [4096, 16], P('fsdp', 'ep'), may hold values from -0.09375 to 0.09375
- router_gain: float32 [4096], P('fsdp'), may hold values from 0.25 to 1.75
Outputs:
- final_down: bfloat16 [16, 6400, 4096], P('ep', 'fsdp')
- scale_down: float32 [16, 6400], P('ep', 'fsdp')
- serve_router: bfloat16 [4096, 16], replicated
All inputs are finite; a program needn't handle non-finite values.
Results may differ from a plain program's by a relative error of at most 0.001.
Values may be sent and summed in bfloat16 or wider, within the bound.
A program may use at most 256 MiB of HBM per device.

v0:
```python
import jax
import jax.numpy as jnp
from jax import lax
from jax.sharding import PartitionSpec as P


def shards(master_down, second_down, router_weight, router_gain):
    merged_down = master_down + second_down.astype(jnp.float32)
    total_down = lax.psum(jnp.sum(merged_down * merged_down, axis=2), "fsdp")
    scale_down = jnp.sqrt(total_down)
    narrow_down = (merged_down / jnp.expand_dims(scale_down, 2)).astype(jnp.bfloat16)
    final_down = lax.all_to_all(narrow_down, "fsdp", split_axis=1, concat_axis=2, tiled=True)
    scale_down = lax.dynamic_slice_in_dim(
        scale_down, lax.axis_index("fsdp") * final_down.shape[1], final_down.shape[1], axis=1
    )
    part_router = (router_weight * router_gain[:, None]).astype(jnp.bfloat16)
    row_router = lax.all_gather(part_router, "fsdp", axis=0, tiled=True)
    serve_router = lax.all_gather(row_router, "ep", axis=1, tiled=True)
    return (final_down, scale_down, serve_router)


def solution(mesh):
    return jax.shard_map(
        shards,
        mesh=mesh,
        in_specs=(P("ep", None, "fsdp"), P("ep", None, "fsdp"), P("fsdp", "ep"), P("fsdp")),
        out_specs=(P("ep", "fsdp", None), P("ep", "fsdp"), P()),
        check_vma=False,
    )
```

profile of v0, /device:TPU:0, one launch (start us, length us, event | category | flops | bytes accessed | tf_op | source)
XLA Modules:
  0.0 905.5 jit_solution(8188198296431997854)
XLA Ops:
  7.2 0.0 all-reduce.2.cloned.1.call-start
  7.2 24.2 %multiply_reduce_fusion = f32[4,6400]{1,0:T(4,128)S(1)} fusion(f32[4,6400,512]{2,1,0:T(8,128)} %param.4, bf16[4,6400,512]{2,1,0:T(8,128)(2,1)} %param.5), kind=kLoop, calls=%fused_computation.1 | loop fusion | flops 52403200 | bytes 78745600 | tf_op jit(solution)/shard_map/reduce_sum | solution.py:9
  31.4 2.3 copy.21
  33.7 0.0 all-reduce.2.cloned.1.call-update
  33.7 135.6 %all-reduce.2.cloned.1.call-done = f32[4,6400]{0,1:T(8,128)} async-done(((f32[4,6400]{0,1:T(8,128)}), f32[4,6400]{0,1:T(8,128)}) %all-reduce.2.cloned.1.call-update) | async-done | bytes 102416 | tf_op jit(solution)/shard_map/psum | solution.py:9
  169.3 2.7 sqrt.3
  172.0 1.2 copy.17
  173.3 34.3 %divide_convert_fusion = bf16[4,6400,512]{2,1,0:T(8,128)(2,1)} fusion(f32[4,6400,512]{2,1,0:T(8,128)} %param.4, bf16[4,6400,512]{2,1,0:T(8,128)(2,1)} %param.5, f32[4,6400]{1,0:T(4,128)S(1)} %copy.17), kind=kLoop, calls=%fused_computation | loop fusion | flops 52428800 | bytes 104960000 | tf_op jit(solution)/shard_map/convert_element_type | solution.py:11
  207.5 33.4 %copy.18 = bf16[4,6400,512]{2,0,1:T(4,128)(2,1)} copy(bf16[4,6400,512]{2,1,0:T(8,128)(2,1)} %divide_convert_fusion) | data formatting | bytes 52428800 | tf_op jit(solution)/shard_map/convert_element_type | solution.py:11
  240.9 0.0 copy-start
  240.9 0.0 copy-start.1
  240.9 6.6 all-to-all-start
  247.6 0.0 copy-done
  247.6 0.0 copy-done.1
  247.6 585.0 %all_gather.6 = bf16[4096,4]{0,1:T(4,128)(2,1)S(1)} all-gather(bf16[512,4]{0,1:T(4,128)(2,1)S(1)} %multiply_convert_fusion), channel_id=1, replica_groups=mesh['ep'=4,'fsdp'=8] {'fsdp'}, dimensions={0}, use_global_device_ids=true | all-gather | bytes 36864 | tf_op jit(solution)/shard_map/all_gather | solution.py:17
  832.7 5.4 all-gather
  838.1 0.7 reshape.9
  838.8 0.8 constant_dynamic-slice_fusion
  839.5 1.8 copy.20
  841.3 0.0 all-to-all-done
  841.3 18.2 %copy.19 = bf16[4,800,8,512]{3,2,1,0:T(8,128)(2,1)} copy(bf16[4,800,8,512]{3,0,1,2:T(4,128)(2,1)} %bitcast.1) | data formatting | bytes 52428800 | tf_op jit(solution)/shard_map/all_to_all | solution.py:12
  859.5 39.2 %all_to_all.16 = bf16[4,800,4096]{2,1,0:T(8,128)(2,1)} reshape(bf16[4,800,8,512]{3,2,1,0:T(8,128)(2,1)} %copy.19) | data formatting | bytes 52428800 | tf_op jit(solution)/shard_map/all_to_all | solution.py:12
  (1 shorter events, 0.0 us)
Async XLA Ops:
  7.2 162.2 %all-reduce.2.cloned.1.call-start = ((), (), s32[]{:S(2)}) async-start(), calls=%async_computation.1 | async-start | bytes 6553600 | tf_op jit(solution)/shard_map/psum | solution.py:9
  240.9 6.7 copy-start
  240.9 6.7 copy-start.1
  240.9 600.4 %all-to-all-start = ((bf16[4,6400,512]{2,0,1:T(4,128)(2,1)}), bf16[4,6400,512]{2,0,1:T(4,128)(2,1)}, u32[]{:S(2)}, u32[]{:S(2)}) async-start(bf16[4,6400,512]{2,0,1:T(4,128)(2,1)} %copy.18), calls=%async_computation | async-start | bytes 52428800 | tf_op jit(solution)/shard_map/all_to_all | solution.py:12
Sparse Core Ops, SparseCore 0:
  33.9 135.4 all-reduce.1
where the time goes:
time: 907 us; the launch traced here: 906 us
  blocking collectives  590 us (65%)
  waiting for transfers between devices  136 us (15%)
  local copies, waits for them, and re-layouts  100 us (11%)
  other arithmetic  58.5 us (6%)
  between operations  14.1 us (2%)
    all_gather x1, blocking collectives, shards(): row_router = lax.all_gather(part_router, 'fsdp', axis=0, tiled=True)  585 us
    psum x1, waiting for transfers between devices, shards(): total_down = lax.psum(jnp.sum(merged_down * merged_down, axis=2), 'fsdp')  136 us
    all_to_all x2, local copies, waits for them, and re-layouts, shards(): lax.all_to_all(narrow_down, 'fsdp', split_axis=1, concat_axis=2, tiled=True)  57.4 us
    convert_element_type x1, other arithmetic, shards(): (merged_down / jnp.expand_dims(scale_down, 2)).astype(jnp.bfloat16)  34.3 us
    convert_element_type x1, local copies, waits for them, and re-layouts, shards(): (merged_down / jnp.expand_dims(scale_down, 2)).astype(jnp.bfloat16)  33.4 us
    reduce_sum x1, other arithmetic, shards(): total_down = lax.psum(jnp.sum(merged_down * merged_down, axis=2), 'fsdp')  24.2 us
  transfers between devices with their start and end apart: 2, of which 1 were waited for; matrix products, arithmetic and copies ran while one was open for 0% of the time, Pallas kernels for 0%

commit v1 on v0

--- a/solution.py
+++ b/solution.py
@@ -6,7 +6,8 @@
 
 def shards(master_down, second_down, router_weight, router_gain):
     merged_down = master_down + second_down.astype(jnp.float32)
-    total_down = lax.psum(jnp.sum(merged_down * merged_down, axis=2), "fsdp")
+    pack_vectors = lambda values: jnp.sum(jax.lax.all_gather(values, "fsdp"), 0)
+    total_down = pack_vectors(jnp.sum(merged_down * merged_down, axis=2))
     scale_down = jnp.sqrt(total_down)
     narrow_down = (merged_down / jnp.expand_dims(scale_down, 2)).astype(jnp.bfloat16)
     final_down = lax.all_to_all(narrow_down, "fsdp", split_axis=1, concat_axis=2, tiled=True)

time: 907 us -> 781 us (0.86)
  waiting for transfers between devices: 136 us -> 0.01 us
  blocking collectives: 590 us -> 620 us
  between operations: 14.1 us -> 0.71 us
    psum x1 -> x0, waiting for transfers between devices: 136 us -> none  [shards(): total_down = lax.psum(jnp.sum(merged_down * merged_down, axis=2), 'fsdp')]
    all_gather x0 -> x1, blocking collectives: none -> 33.9 us  [shards(): pack_vectors = lambda values: jnp.sum(jax.lax.all_gather(values, 'fsdp'), 0)]
    reduce_sum x1 -> x2, other arithmetic: 24.2 us -> 24.4 us  [the longest x1 24.2 us: shards(): total_down = pack_vectors(jnp.sum(merged_down * merged_down, axis=2))]
  transfers between devices with their start and end apart: 2 -> 1, of which waited for: 1 -> 0; matrix products, arithmetic and copies ran while one was open for 0% -> 0% of each run, Pallas kernels for 0% -> 0%
where the time goes in v1:
time: 781 us; the launch traced here: 780 us
  blocking collectives  620 us (79%)
  local copies, waits for them, and re-layouts  94.5 us (12%)
  other arithmetic  58.7 us (8%)
    all_gather x1, blocking collectives, shards(): row_router = lax.all_gather(part_router, 'fsdp', axis=0, tiled=True)  580 us
    all_to_all x2, local copies, waits for them, and re-layouts, shards(): lax.all_to_all(narrow_down, 'fsdp', split_axis=1, concat_axis=2, tiled=True)  57.4 us
    convert_element_type x1, other arithmetic, shards(): (merged_down / jnp.expand_dims(scale_down, 2)).astype(jnp.bfloat16)  34.3 us
    all_gather x1, blocking collectives, shards(): pack_vectors = lambda values: jnp.sum(jax.lax.all_gather(values, 'fsdp'), 0)  33.9 us
    convert_element_type x1, local copies, waits for them, and re-layouts, shards(): (merged_down / jnp.expand_dims(scale_down, 2)).astype(jnp.bfloat16)  33.4 us
    reduce_sum x1, other arithmetic, shards(): total_down = pack_vectors(jnp.sum(merged_down * merged_down, axis=2))  24.2 us
  transfers between devices with their start and end apart: 1, of which 0 were waited for; matrix products, arithmetic and copies ran while one was open for 0% of the time, Pallas kernels for 0%

profile of v1, /device:TPU:0, one launch (start us, length us, event | category | flops | bytes accessed | tf_op | source)
XLA Modules:
  0.0 780.0 jit_solution(1847130021066882002)
XLA Ops:
  0.6 24.2 %multiply_reduce_fusion = f32[4,6400]{1,0:T(4,128)S(1)} fusion(f32[4,6400,512]{2,1,0:T(8,128)} %param.4, bf16[4,6400,512]{2,1,0:T(8,128)(2,1)} %param.5), kind=kLoop, calls=%fused_computation.1 | loop fusion | flops 52403200 | bytes 78745600 | tf_op jit(solution)/shard_map/reduce_sum | solution.py:10
  24.9 1.1 copy.21
  26.0 1.2 copy.18
  27.2 33.9 %all-gather.1 = f32[8,4,6400]{2,1,0:T(4,128)S(1)} all-gather(f32[1,4,6400]{2,1,0:T(4,128)S(1)} %copy.18), channel_id=2, replica_groups=mesh['ep'=4,'fsdp'=8] {'fsdp'}, dimensions={0}, use_global_device_ids=true | all-gather | bytes 921600 | tf_op jit(solution)/shard_map/all_gather | solution.py:9
  61.2 0.1 reduce_sum.19
  61.3 0.1 sqrt.7
  61.4 34.3 %divide_convert_fusion = bf16[4,6400,512]{2,1,0:T(8,128)(2,1)} fusion(f32[4,6400,512]{2,1,0:T(8,128)} %param.4, bf16[4,6400,512]{2,1,0:T(8,128)(2,1)} %param.5, f32[4,6400]{1,0:T(4,128)S(1)} %sqrt.7), kind=kLoop, calls=%fused_computation | loop fusion | flops 52428800 | bytes 104960000 | tf_op jit(solution)/shard_map/convert_element_type | solution.py:12
  95.6 0.0 copy-start
  95.6 0.0 copy-start.1
  95.7 33.4 %copy.19 = bf16[4,6400,512]{2,0,1:T(4,128)(2,1)} copy(bf16[4,6400,512]{2,1,0:T(8,128)(2,1)} %divide_convert_fusion) | data formatting | bytes 52428800 | tf_op jit(solution)/shard_map/convert_element_type | solution.py:12
  129.0 6.5 all-to-all-start
  135.5 0.0 copy-done
  135.6 0.0 copy-done.1
  135.6 580.2 %all_gather.14 = bf16[4096,4]{0,1:T(4,128)(2,1)S(1)} all-gather(bf16[512,4]{0,1:T(4,128)(2,1)S(1)} %multiply_convert_fusion), channel_id=1, replica_groups=mesh['ep'=4,'fsdp'=8] {'fsdp'}, dimensions={0}, use_global_device_ids=true | all-gather | bytes 36864 | tf_op jit(solution)/shard_map/all_gather | solution.py:18
  715.8 5.4 all-gather.2
  721.2 0.7 reshape.14
  721.9 0.7 constant_dynamic-slice_fusion
  722.6 0.0 all-to-all-done
  722.6 18.2 %copy.20 = bf16[4,800,8,512]{3,2,1,0:T(8,128)(2,1)} copy(bf16[4,800,8,512]{3,0,1,2:T(4,128)(2,1)} %bitcast.2) | data formatting | bytes 52428800 | tf_op jit(solution)/shard_map/all_to_all | solution.py:13
  740.8 39.2 %all_to_all.16 = bf16[4,800,4096]{2,1,0:T(8,128)(2,1)} reshape(bf16[4,800,8,512]{3,2,1,0:T(8,128)(2,1)} %copy.20) | data formatting | bytes 52428800 | tf_op jit(solution)/shard_map/all_to_all | solution.py:13
  (1 shorter events, 0.0 us)
Async XLA Ops:
  95.6 39.9 %copy-start = (f32[512,4]{0,1:T(4,128)S(1)}, f32[512,4]{0,1:T(4,128)}, u32[]{:S(2)}) copy-start(f32[512,4]{0,1:T(4,128)} %param.6) | copy-start | bytes 24580
  95.6 39.9 %copy-start.1 = (f32[512]{0:T(512)S(1)}, f32[512]{0:T(512)}, u32[]{:S(2)}) copy-start(f32[512]{0:T(512)} %param.7) | copy-start | bytes 6148
  129.0 593.6 %all-to-all-start = ((bf16[4,6400,512]{2,0,1:T(4,128)(2,1)}), bf16[4,6400,512]{2,0,1:T(4,128)(2,1)}, u32[]{:S(2)}, u32[]{:S(2)}) async-start(bf16[4,6400,512]{2,0,1:T(4,128)(2,1)} %copy.19), calls=%async_computation | async-start | bytes 52428800 | tf_op jit(solution)/shard_map/all_to_all | solution.py:13
